TPU v7x, 32 devices: a whole 2x2x4 slice. The times are simulated.
32 devices in a mesh: tile: 8 (over z, x), mem: 4 (over y, core).
Axes of the slice: x: 2, y: 2, z: 4, core: 2. Of those that a mesh axis runs over, the one named last changes fastest.
Arguments:
- footprints: bfloat16 [1024, 128, 128], P('tile'), may hold values from -0.1875 to 0.1875
- tile_row: int32 [1024], P('tile'), may hold values from 0 to 127, as said below
- tile_col: int32 [1024], P('tile'), may hold values from 0 to 63, as said below
- prior_flux: bfloat16 [256, 8192], P('mem', 'tile'), may hold values from -12 to 12
- observed: float32 [256, 16384], P('mem', 'tile'), may hold values from -6 to 6
- precision_weight: int32 [16384], P('tile'), may hold values from 1 to 16
Outputs:
- gradient: float32 [256, 8192], P('mem', 'tile')
Inputs may be any that keep to these rules, and one draw needn't show every extreme that they name: Among the 128 tiles of each index of tile, at most 24 have a row block of one owner (owner = tile_row // 16); in every draw one owner gets exactly 24 from every index. Likewise with owner = tile_col // 8: at most 24 from one index of tile to one owner, and one owner gets exactly 24 from every index.
All inputs are finite; a program needn't handle non-finite values.
Results may differ from a plain program's by a relative error of at most 0.0052.
Values may be sent and summed in bfloat16 or wider, within the bound.
No kernel may reach another device: no remote copies, remote signals or barrier semaphores. Data moves between devices by JAX's collectives and lax.ppermute only.
A program may use at most 64 MiB of HBM per device.

v0:
```python
import jax
import jax.numpy as jnp
from jax import lax
from jax.sharding import PartitionSpec as P

MEMBERS = 256
FLUX_DEV = 8
SOUND_DEV = 16


def slot_of(owners, capacity):
    entries = owners.shape[0]
    position = jnp.arange(entries)
    earlier = (owners[:, None] == owners[None, :]) & (position[None, :] < position[:, None])
    return owners * capacity + jnp.sum(earlier.astype(jnp.int32), axis=1)


def invert(slot_ids, slot_total):
    matches = slot_ids[None, :] == jnp.arange(slot_total)[:, None]
    sources = jnp.sum(jnp.where(matches, jnp.arange(slot_ids.shape[0])[None, :], 0), axis=1)
    return (sources, jnp.any(matches, axis=1))


def to_slots(values, sources, usage_flags):
    placed = jnp.take(values, sources, axis=1)
    return jnp.where(usage_flags[None, :, None], placed, jnp.zeros_like(placed))


def body(footprints, tile_row, tile_col, prior_flux, observed, precision_weight):
    devices_tile = lax.axis_size("tile")
    tile_count = footprints.shape[0]
    tile_size = footprints.shape[1]
    capacity = tile_count // devices_tile + max(1, tile_count // (2 * devices_tile))
    slot_total = devices_tile * capacity
    local_members = prior_flux.shape[0]
    local_sum = jnp.sum(prior_flux.astype(jnp.float32), axis=0)
    ensemble_sum = lax.psum(local_sum, "mem")
    ensemble_mean = ensemble_sum / MEMBERS
    member_deviations = (prior_flux.astype(jnp.float32) - ensemble_mean[None, :]).astype(
        jnp.bfloat16
    )
    row_owner = tile_row // SOUND_DEV
    row_local = tile_row % SOUND_DEV
    row_slot = slot_of(row_owner, capacity)
    row_source, row_used = invert(row_slot, slot_total)
    gathered = lax.all_gather(member_deviations, "tile", axis=1, tiled=True)
    retrieved_blocks = jnp.take(gathered.reshape(local_members, -1, tile_size), tile_col, axis=1)
    forward_terms = jnp.einsum(
        "mtk,trk->mtr", retrieved_blocks, footprints, preferred_element_type=jnp.float32
    )
    row_index = jnp.where(row_used, jnp.take(row_local, row_source), SOUND_DEV)
    sent_terms = to_slots(forward_terms, row_source, row_used)
    got_terms, got_rows = (
        lax.all_to_all(sent_terms, "tile", split_axis=1, concat_axis=1, tiled=True),
        lax.all_to_all(row_index[None, :], "tile", split_axis=1, concat_axis=1, tiled=True),
    )
    got_rows = got_rows[0]
    row_match = (got_rows[None, :] == jnp.arange(SOUND_DEV)[:, None]).astype(jnp.float32)
    modelled = jnp.einsum("ds,msk->mdk", row_match, got_terms, precision=lax.Precision.HIGHEST)
    targets = observed.reshape(local_members, SOUND_DEV, tile_size)
    obs_weight = (precision_weight.astype(jnp.float32) / 8.0).reshape(SOUND_DEV, tile_size)
    weighted = (obs_weight[None, :, :] * (modelled - targets)).astype(jnp.bfloat16)
    reply_rows = jnp.take(weighted, jnp.minimum(got_rows, SOUND_DEV - 1), axis=1)
    returned = lax.all_to_all(reply_rows, "tile", split_axis=1, concat_axis=1, tiled=True)
    residual_tiles = jnp.take(returned, row_slot, axis=1)
    backward_terms = jnp.einsum(
        "mtr,trk->mtk", residual_tiles, footprints, preferred_element_type=jnp.float32
    )
    picked = (tile_col[None, :] == jnp.arange(lax.axis_size("tile") * FLUX_DEV)[:, None]).astype(
        jnp.float32
    )
    reduced_total = lax.psum_scatter(
        jnp.einsum("ct,mtk->cmk", picked, backward_terms, precision=lax.Precision.HIGHEST),
        "tile",
        scatter_dimension=0,
        tiled=True,
    )
    gradient = reduced_total.transpose(1, 0, 2).reshape(local_members, FLUX_DEV * tile_size)
    return gradient


def solution(mesh):
    in_specs = (
        P("tile", None, None),
        P("tile"),
        P("tile"),
        P("mem", "tile"),
        P("mem", "tile"),
        P("tile"),
    )
    out_specs = P("mem", "tile")
    return jax.shard_map(body, mesh=mesh, in_specs=in_specs, out_specs=out_specs, check_vma=False)
```

profile of v0, /device:TPU:0, one launch (start us, length us, event | category | flops | bytes accessed | tf_op | source)
XLA Modules:
  0.0 394.9 jit_solution(9114734959783431947)
XLA Ops:
  6.5 0.9 convert_reduce_fusion
  7.5 8.4 %psum.7 = f32[1024]{0:T(1024)S(1)} all-reduce(f32[1024]{0:T(1024)S(1)} %convert_reduce_fusion), channel_id=1, replica_groups=mesh['tile'=8,'mem'=4] {'mem'}, use_global_device_ids=true, to_apply=%region_4.5 | all-reduce | flops 1024 | bytes 8192 | tf_op jit(solution)/shard_map/psum | solution.py:37
  15.9 1.6 fusion.24
  17.5 0.7 and_select_fusion
  18.2 0.2 convert_reduce_fusion.1
  18.4 0.1 select_reduce_fusion
  18.6 1.6 gather_fusion
  20.2 0.1 fusion.25
  20.4 0.6 select_select_fusion
  21.0 5.8 %all-to-all-start = ((s32[1,8,24]{2,0,1:T(1,128)}), s32[1,8,24]{2,0,1:T(1,128)S(1)}, u32[]{:S(2)}, u32[]{:S(2)}) async-start(s32[1,8,24]{2,0,1:T(1,128)} %bitcast.3), calls=%async_computation | async-start | bytes 8192 | tf_op jit(solution)/shard_map/all_to_all | solution.py:55
  26.8 0.7 compare_select_fusion.5
  27.5 0.7 compare_and_fusion
  28.2 30.0 %all-gather.2.cloned.1.call-done = bf16[64,8192]{1,0:T(8,128)(2,1)} async-done(((bf16[64,1024]{1,0:T(8,128)(2,1)}), bf16[64,8192]{1,0:T(8,128)(2,1)}) %all-gather.2.cloned.1.call-update) | async-done | bytes 1048592 | tf_op jit(solution)/shard_map/all_gather | solution.py:46
  58.2 1.5 copy_bitcast_fusion
  59.7 1.0 gather_fusion.1
  60.7 7.0 %convolution_bitcast_fusion.1 = f32[64,128,128]{2,0,1:T(8,128)} fusion(bf16[128,128,128]{2,1,0:T(8,128)(2,1)} %param.6, bf16[128,64,128]{2,1,0:T(8,128)(2,1)S(1)} %gather_fusion.1, pred[128]{0:T(512)(128)(4,1)S(1)} %compare_and_fusion), kind=kOutput, calls=%fused_computation.12 | convolution fusion | flops 269484032 | bytes 10485888 | tf_op jit(solution)/shard_map/mtk,trk->mtr/dot_general | solution.py:48
  67.7 5.8 %gather_fusion.2 = f32[192,64,128]{2,1,0:T(8,128)} fusion(f32[64,128,128]{2,0,1:T(8,128)} %convolution_bitcast_fusion.1, s32[1024]{0:T(1024)S(1)} %pad_clamp_fusion.3), kind=kCustom, calls=%fused_computation.2 | custom fusion | bytes 12583680 | tf_op jit(solution)/shard_map/jit(_take)/gather | solution.py:25
  73.5 5.4 %select_bitcast_fusion = f32[64,192,128]{2,0,1:T(8,128)} fusion(f32[192,64,128]{2,1,0:T(8,128)} %gather_fusion.2, pred[192]{0:T(512)(128)(4,1)S(1)} %fusion.25, pred[192]{0:T(512)(128)(4,1)S(1)} %compare_and_fusion.1), kind=kLoop, calls=%fused_computation.7 | loop fusion | flops 3145728 | bytes 12583296 | tf_op jit(solution)/shard_map/jit(_where)/select_n | solution.py:26
  79.0 4.9 %all-to-all-start.1 = ((f32[64,192,128]{2,0,1:T(8,128)}), f32[64,192,128]{2,0,1:T(8,128)}, u32[]{:S(2)}, u32[]{:S(2)}) async-start(f32[64,192,128]{2,0,1:T(8,128)} %select_bitcast_fusion), calls=%async_computation.1 | async-start | bytes 12582912 | tf_op jit(solution)/shard_map/all_to_all | solution.py:54
  84.0 0.5 broadcast.213
  84.5 0.7 minimum_reduce_fusion
  85.4 135.2 %all-to-all-done.1 = f32[64,192,128]{2,0,1:T(8,128)} async-done(((f32[64,192,128]{2,0,1:T(8,128)}), f32[64,192,128]{2,0,1:T(8,128)}, u32[]{:S(2)}, u32[]{:S(2)}) %all-to-all-start.1) | async-done | bytes 6291488 | tf_op jit(solution)/shard_map/all_to_all | solution.py:54
  220.6 8.1 %fusion.19 = bf16[64,16,128]{2,1,0:T(8,128)(2,1)S(1)} fusion(f32[64,16,128]{2,1,0:T(8,128)S(1)} %bitcast.49, f32[64,192,128]{2,0,1:T(8,128)} %all-to-all-done.1, f32[16,128]{1,0:T(8,128)S(1)} %multiply_bitcast_fusion, s32[192]{0:T(256)S(1)} %squeeze.3), kind=kOutput, calls=%fused_computation.22 | convolution fusion | flops 302386176 | bytes 7086848 | tf_op jit(solution)/shard_map/ds,msk->mdk/dot_general | solution.py:59
  228.7 1.2 gather_fusion.3
  229.9 2.1 select_bitcast_fusion.1
  232.0 3.6 all-to-all-start.2
  235.7 70.8 %all-to-all-done.2 = bf16[64,192,128]{2,0,1:T(8,128)(2,1)S(1)} async-done(((bf16[64,192,128]{2,0,1:T(8,128)(2,1)}), bf16[64,192,128]{2,0,1:T(8,128)(2,1)S(1)}, u32[]{:S(2)}, u32[]{:S(2)}) %all-to-all-start.2) | async-done | bytes 3145760 | tf_op jit(solution)/shard_map/all_to_all | solution.py:64
  306.5 2.2 gather_fusion.4
  308.7 4.1 %convolution_bitcast_fusion = f32[64,128,128]{2,0,1:T(8,128)S(1)} fusion(bf16[128,128,128]{2,1,0:T(8,128)(2,1)} %param.6, bf16[128,64,128]{2,1,0:T(8,128)(2,1)} %gather_fusion.4, pred[128]{0:T(512)(128)(4,1)S(1)} %get-tuple-element.7), kind=kOutput, calls=%fused_computation.11 | convolution fusion | flops 269484032 | bytes 10485888 | tf_op jit(solution)/shard_map/mtr,trk->mtk/dot_general | solution.py:66
  312.8 5.4 %fusion.2 = f32[64,64,128]{2,0,1:T(8,128)} fusion(f32[64,128,128]{2,0,1:T(8,128)S(1)} %convolution_bitcast_fusion, s32[128]{0:T(128)S(1)} %copy-done.2), kind=kOutput, calls=%fused_computation.8 | convolution fusion | flops 805314560 | bytes 6291968 | tf_op jit(solution)/shard_map/ct,mtk->cmk/dot_general | solution.py:73
  318.3 68.2 %reduce-scatter.2.cloned.1.call-done = f32[8,64,128]{2,0,1:T(8,128)} async-done(((f32[64,64,128]{2,0,1:T(8,128)}), f32[8,64,128]{2,0,1:T(8,128)}) %reduce-scatter.2.cloned.1.call-update) | async-done | bytes 262160 | tf_op jit(solution)/shard_map/reduce_scatter | solution.py:72
  386.4 1.7 copy.42
  (30 shorter events, 0.7 us)
Async XLA Ops:
  6.5 51.7 %all-gather.2.cloned.1.call-start = ((), (), s32[]{:S(2)}) async-start(), calls=%async_computation.4 | async-start | bytes 1179648 | tf_op jit(solution)/shard_map/all_gather | solution.py:46
  21.0 57.9 %all-to-all-start = ((s32[1,8,24]{2,0,1:T(1,128)}), s32[1,8,24]{2,0,1:T(1,128)S(1)}, u32[]{:S(2)}, u32[]{:S(2)}) async-start(s32[1,8,24]{2,0,1:T(1,128)} %bitcast.3), calls=%async_computation | async-start | bytes 8192 | tf_op jit(solution)/shard_map/all_to_all | solution.py:55
  79.0 4.9 %copy-start = (f32[64,2048]{1,0:T(8,128)S(1)}, f32[64,2048]{1,0:T(8,128)}, u32[]{:S(2)}) copy-start(f32[64,2048]{1,0:T(8,128)} %param.10) | copy-start | bytes 1572868
  79.0 5.0 %copy-start.1 = (s32[2048]{0:T(1024)S(1)}, s32[2048]{0:T(1024)}, u32[]{:S(2)}) copy-start(s32[2048]{0:T(1024)} %param.11) | copy-start | bytes 24580
  79.0 141.6 %all-to-all-start.1 = ((f32[64,192,128]{2,0,1:T(8,128)}), f32[64,192,128]{2,0,1:T(8,128)}, u32[]{:S(2)}, u32[]{:S(2)}) async-start(f32[64,192,128]{2,0,1:T(8,128)} %select_bitcast_fusion), calls=%async_computation.1 | async-start | bytes 12582912 | tf_op jit(solution)/shard_map/all_to_all | solution.py:54
  232.0 74.5 %all-to-all-start.2 = ((bf16[64,192,128]{2,0,1:T(8,128)(2,1)}), bf16[64,192,128]{2,0,1:T(8,128)(2,1)S(1)}, u32[]{:S(2)}, u32[]{:S(2)}) async-start(bf16[64,192,128]{2,0,1:T(8,128)(2,1)} %select_bitcast_fusion.1), calls=%async_computation.2 | async-start | bytes 6291456 | tf_op jit(solution)/shard_map/all_to_all | solution.py:64
  235.6 150.8 %reduce-scatter.2.cloned.1.call-start = ((), (), s32[]{:S(2)}) async-start(), calls=%async_computation.5 | async-start | bytes 2359296 | tf_op jit(solution)/shard_map/reduce_scatter | solution.py:72
  308.7 4.1 %copy-start.2 = (s32[128]{0:T(128)S(1)}, s32[128]{0:T(128)}, u32[]{:S(2)}) copy-start(s32[128]{0:T(128)} %param.8) | copy-start | bytes 1540
Sparse Core Ops, SparseCore 0:
  17.6 40.5 all-gather.1
  318.4 67.9 reduce-scatter.1
where the time goes:
time: 396 us; the launch traced here: 395 us
  waiting for transfers between devices  304 us (77%)
  matrix products  24.7 us (6%)
  local copies, waits for them, and re-layouts  15.9 us (4%)
  starting transfers between devices  14.4 us (4%)
  other arithmetic  13.8 us (3%)
  between operations  13.6 us (3%)
  blocking collectives  8.4 us (2%)
    all_to_all x1, waiting for transfers between devices, body(): lax.all_to_all(sent_terms, 'tile', split_axis=1, concat_axis=1, tiled=True)  135 us
    all_to_all x1, waiting for transfers between devices, body(): lax.all_to_all(reply_rows, 'tile', split_axis=1, concat_axis=1, tiled=True)  70.8 us
    reduce_scatter x1, waiting for transfers between devices, body(): lax.psum_scatter(jnp.einsum('ct,mtk->cmk', picked, backward_terms, precis...  68.2 us
    all_gather x1, waiting for transfers between devices, body(): gathered = lax.all_gather(member_deviations, 'tile', axis=1, tiled=True)  30 us
    psum x1, blocking collectives, body(): ensemble_sum = lax.psum(local_sum, 'mem')  8.4 us
    dot_general x1, matrix products, body(): jnp.einsum('ds,msk->mdk', row_match, got_terms, precision=lax.Precision.H...  8.12 us
  transfers between devices with their start and end apart: 5, of which 4 were waited for; matrix products, arithmetic and copies ran while one was open for 7% of the time, Pallas kernels for 0%

commit v1 on v0

v1 whole, which is shorter than its diff:
```python
import jax
import jax.numpy as jnp
from jax import lax
from jax.experimental import pallas as pl
from jax.experimental.pallas import tpu as pltpu
from jax.sharding import PartitionSpec as P


def rank_in_owner(owners):
    position = jnp.arange(owners.shape[0])
    earlier = (owners[:, None] == owners[None, :]) & (position[None, :] < position[:, None])
    return jnp.sum(earlier.astype(jnp.int32), axis=1)


def exchange(value, axis, distance):
    size = lax.axis_size(axis)
    return lax.ppermute(value, axis, [(i, i ^ distance) for i in range(size)])


def distances(size):
    found = []
    step = size // 2
    while step:
        found.append(step)
        step //= 2
    return found


def local_kernel(rows, cols, *refs, quarters, unroll):
    tiles = refs[:quarters]
    flux, observed, weight, near, far, modelled, weighted, total = refs[quarters:]
    soundings = modelled.shape[0] - 1
    cells = total.shape[0] - 1
    side = flux.shape[2]
    per_quarter = tiles[0].shape[0]
    modelled[...] = jnp.zeros_like(modelled)
    total[...] = jnp.zeros_like(total)

    for q in range(quarters):

        def forward(step, carry, q=q):
            terms = []
            for u in range(unroll):
                t = step * unroll + u
                c = jnp.minimum(cols[q * per_quarter + t], cells - 1)
                terms.append(
                    lax.dot_general(
                        flux[c], tiles[q][t], (((1,), (1,)), ((), ())), preferred_element_type=jnp.float32
                    )
                )
            for u in range(unroll):
                r = rows[q * per_quarter + step * unroll + u]
                modelled[r] = modelled[r] + terms[u]
            return carry

        lax.fori_loop(0, per_quarter // unroll, forward, 0)

    scale = weight[...].astype(jnp.float32) / 8.0
    for r in range(soundings):
        part = slice(r * side, (r + 1) * side)
        weighted[r] = (scale[:, part] * (modelled[r] - observed[:, part])).astype(jnp.bfloat16)
    weighted[soundings] = jnp.zeros_like(weighted[soundings])

    for q in range(quarters):

        def backward(step, carry, q=q):
            terms = []
            for u in range(unroll):
                t = step * unroll + u
                r = rows[q * per_quarter + t]
                terms.append(jnp.dot(weighted[r], tiles[q][t], preferred_element_type=jnp.float32))
            for u in range(unroll):
                c = cols[q * per_quarter + step * unroll + u]
                total[c] = total[c] + terms[u]
            return carry

        lax.fori_loop(0, per_quarter // unroll, backward, 0)

    half = cells // 2
    near[...] = total[:half]
    far[...] = total[half:cells].astype(jnp.bfloat16)


def body(footprints, tile_row, tile_col, prior_flux, observed, precision_weight):
    devices_tile = lax.axis_size("tile")
    devices_mem = lax.axis_size("mem")
    me = lax.axis_index("tile")
    quarter = lax.axis_index("mem")
    tile_count, side, _ = footprints.shape
    local_members = prior_flux.shape[0]
    members = local_members * devices_mem
    flux_local = prior_flux.shape[1] // side
    sound_local = observed.shape[1] // side
    flux_all = flux_local * devices_tile

    capacity = tile_count // devices_tile + max(1, tile_count // (2 * devices_tile))
    share = -(-capacity // devices_mem)
    capacity = share * devices_mem
    owner = tile_row // sound_local
    slot = owner * capacity + rank_in_owner(owner)
    hit = slot[None, :] == jnp.arange(devices_tile * capacity)[:, None]
    source = jnp.sum(jnp.where(hit, jnp.arange(tile_count)[None, :], 0), axis=1)
    code = (tile_row % sound_local) * flux_all + tile_col
    codes = jnp.sum(jnp.where(hit, code[None, :] + 1, 0), axis=1) - 1
    mine = lax.dynamic_slice_in_dim(source.reshape(devices_tile, capacity), quarter * share, share, axis=1)
    sent = jnp.take(footprints, mine.reshape(-1), axis=0)
    got = lax.all_to_all(sent, "tile", split_axis=0, concat_axis=0, tiled=True)
    got_codes = lax.all_to_all(
        codes.reshape(devices_tile, capacity), "tile", split_axis=0, concat_axis=0, tiled=True
    )
    quarters = [got]
    steps = distances(devices_mem)
    for distance in steps:
        quarters = quarters + [exchange(q, "mem", distance) for q in quarters]
    order = [0]
    for distance in steps:
        order = order + [q ^ distance for q in order]

    by_share = got_codes.reshape(devices_tile, devices_mem, share)
    table = jnp.stack([jnp.take(by_share, quarter ^ q, axis=1) for q in order]).reshape(-1)
    used = table >= 0
    col = jnp.where(used, table % flux_all, 0)
    relative = (col // flux_local) ^ me
    place = jnp.zeros_like(relative)
    for i, distance in enumerate(distances(devices_tile)):
        place = place + (((relative // distance) & 1) << i)
    rows = jnp.where(used, table // flux_all, sound_local)
    cols = jnp.where(used, place * flux_local + col % flux_local, flux_all)

    prior = prior_flux.astype(jnp.float32)
    total = jnp.sum(prior, axis=0, keepdims=True)
    for distance in reversed(distances(devices_mem)):
        total = total + exchange(total, "mem", distance)
    anomalies = (prior - total / members).astype(jnp.bfloat16)
    flux = anomalies.reshape(local_members, flux_local, side).transpose(1, 0, 2)
    for distance in distances(devices_tile):
        flux = jnp.concatenate([flux, exchange(flux, "tile", distance)], axis=0)

    unroll = 8
    while got.shape[0] % unroll:
        unroll //= 2
    vmem = pl.BlockSpec(memory_space=pltpu.VMEM)
    smem = pl.BlockSpec(memory_space=pltpu.SMEM)
    near, far = pl.pallas_call(
        lambda *refs: local_kernel(*refs, quarters=devices_mem, unroll=unroll),
        out_shape=(
            jax.ShapeDtypeStruct((flux_all // 2, local_members, side), jnp.float32),
            jax.ShapeDtypeStruct((flux_all // 2, local_members, side), jnp.bfloat16),
        ),
        in_specs=[smem, smem] + [vmem] * (devices_mem + 3),
        out_specs=(vmem, vmem),
        scratch_shapes=[
            pltpu.VMEM((sound_local + 1, local_members, side), jnp.float32),
            pltpu.VMEM((sound_local + 1, local_members, side), jnp.bfloat16),
            pltpu.VMEM((flux_all + 1, local_members, side), jnp.float32),
        ],
        name="local_adjoint",
    )(rows, cols, *quarters, flux, observed, precision_weight.reshape(1, -1))

    for distance in reversed(distances(devices_tile)):
        near = near + exchange(far, "tile", distance).astype(jnp.float32)
        if distance < devices_tile // 2:
            half = near.shape[0] // 2
            near, far = near[:half], near[half:].astype(jnp.bfloat16)
    return near.transpose(1, 0, 2).reshape(local_members, flux_local * side)


def solution(mesh):
    in_specs = (
        P("tile", None, None),
        P("tile"),
        P("tile"),
        P("mem", "tile"),
        P("mem", "tile"),
        P("tile"),
    )
    return jax.shard_map(body, mesh=mesh, in_specs=in_specs, out_specs=P("mem", "tile"), check_vma=False)
```

time: 396 us -> 167 us (0.42)
  waiting for transfers between devices: 304 us -> 80.1 us
  blocking collectives: 8.4 us -> 44.2 us
  matrix products: 24.7 us -> 0 us
  Pallas kernels: 0 us -> 16.7 us
  between operations: 13.6 us -> 0.25 us
  local copies, waits for them, and re-layouts: 15.9 us -> 5.51 us
  other arithmetic: 13.8 us -> 7.91 us
    all_to_all x3 -> x1, waiting for transfers between devices: 206 us -> 7.74 us  [body(): lax.all_to_all(codes.reshape(devices_tile, capacity), 'tile', split_axis=...]
    ppermute x0 -> x11, waiting for transfers between devices: none -> 72.4 us  [exchange(): return lax.ppermute(value, axis, [(i, i ^ distance) for i in range(size)])]
    reduce_scatter x1 -> x0, waiting for transfers between devices: 68.2 us -> none  [body(): lax.psum_scatter(jnp.einsum('ct,mtk->cmk', picked, backward_terms, precis...]
    all_to_all x0 -> x1, blocking collectives: none -> 44.2 us  [body(): got = lax.all_to_all(sent, 'tile', split_axis=0, concat_axis=0, tiled=True)]
    all_gather x1 -> x0, waiting for transfers between devices: 30 us -> none  [body(): gathered = lax.all_gather(member_deviations, 'tile', axis=1, tiled=True)]
    dot_general x4 -> x0, matrix products: 24.7 us -> none  [the longest x1 8.12 us: body(): jnp.einsum('ds,msk->mdk', row_match, got_terms, precision=lax.Precision.H...]
    pallas_call x0 -> x1, Pallas kernels: none -> 16.7 us  [body(): pl.pallas_call(lambda *refs: local_kernel(*refs, quarters=devices_mem, un...]
    all_to_all x3 -> x1, starting transfers between devices: 14.3 us -> 3.26 us  [body(): lax.all_to_all(codes.reshape(devices_tile, capacity), 'tile', split_axis=...]
  transfers between devices with their start and end apart: 5 -> 12, of which waited for: 4 -> 8; matrix products, arithmetic and copies ran while one was open for 7% -> 4% of each run, Pallas kernels for 0% -> 0%
where the time goes in v1:
time: 167 us
  waiting for transfers between devices  80.1 us (48%)
  blocking collectives  44.2 us (26%)
  Pallas kernels  16.7 us (10%)
  starting transfers between devices  11.8 us (7%)
  other arithmetic  7.91 us (5%)
  local copies, waits for them, and re-layouts  5.51 us (3%)
    ppermute x11, waiting for transfers between devices, exchange(): return lax.ppermute(value, axis, [(i, i ^ distance) for i in range(size)])  72.4 us
    all_to_all x1, blocking collectives, body(): got = lax.all_to_all(sent, 'tile', split_axis=0, concat_axis=0, tiled=True)  44.2 us
    pallas_call x1, Pallas kernels, body(): pl.pallas_call(lambda *refs: local_kernel(*refs, quarters=devices_mem, un...  16.7 us
    ppermute x11, starting transfers between devices, exchange(): return lax.ppermute(value, axis, [(i, i ^ distance) for i in range(size)])  8.54 us
    all_to_all x1, waiting for transfers between devices, body(): lax.all_to_all(codes.reshape(devices_tile, capacity), 'tile', split_axis=...  7.74 us
  transfers between devices with their start and end apart: 12, of which 8 were waited for; matrix products, arithmetic and copies ran while one was open for 4% of the time, Pallas kernels for 0%

profile of v1, /device:TPU:0, one launch (start us, length us, event | category | flops | bytes accessed | tf_op | source)
XLA Modules:
  0.0 166.5 jit_solution(6170727938565585491)
XLA Ops:
  0.0 0.7 fusion.11
  0.7 0.2 convert_reduce_fusion.1
  1.4 3.0 %gather_fusion = bf16[48,128,128]{2,1,0:T(8,128)(2,1)S(1)} fusion(bf16[128,128,128]{2,1,0:T(8,128)(2,1)} %param.8, s32[1024]{0:T(1024)S(1)} %pad_clamp_fusion), kind=kCustom, calls=%fused_computation | custom fusion | bytes 3145920 | tf_op jit(solution)/shard_map/jit(_take)/gather | solution.py:106
  4.4 0.2 broadcast_select_fusion
  4.7 44.2 %all_to_all.11.refs_2_ = bf16[48,128,128]{2,1,0:T(8,128)(2,1)S(1)} all-to-all(bf16[48,128,128]{2,1,0:T(8,128)(2,1)S(1)} %broadcast_select_fusion), channel_id=1, replica_groups=mesh['tile'=8,'mem'=4] {'tile'}, dimensions={0} | all-to-all | bytes 3145728 | tf_op jit(solution)/shard_map/all_to_all | solution.py:107
  48.9 1.5 collective-permute-start
  50.5 1.2 collective-permute-done.3
  51.7 0.5 collective-permute-start.4
  52.2 31.7 %collective-permute-done.4 = f32[1,1024]{1,0:T(1,128)S(1)} collective-permute-done((f32[1,1024]{1,0:T(1,128)S(1)}, f32[1,1024]{1,0:T(1,128)S(1)}, u32[]{:S(2)}, u32[]{:S(2)}) %collective-permute-start.4) | collective-permute-done | bytes 4128 | tf_op jit(solution)/shard_map/ppermute | solution.py:17
  84.0 0.5 collective-permute-start.2
  84.5 1.5 collective-permute-start.5
  86.1 7.7 %collective-permute-done.5 = bf16[8,64,128]{2,1,0:T(8,128)(2,1)S(1)} collective-permute-done((bf16[8,64,128]{2,1,0:T(8,128)(2,1)S(1)}, bf16[8,64,128]{2,1,0:T(8,128)(2,1)S(1)}, u32[]{:S(2)}, u32[]{:S(2)}) %collective-permute-start.5) | collective-permute-done | bytes 131104 | tf_op jit(solution)/shard_map/ppermute | solution.py:17
  93.9 8.0 %collective-permute-done.6 = bf16[16,64,128]{2,1,0:T(8,128)(2,1)S(1)} collective-permute-done((bf16[16,64,128]{2,1,0:T(8,128)(2,1)S(1)}, bf16[16,64,128]{2,1,0:T(8,128)(2,1)S(1)}, u32[]{:S(2)}, u32[]{:S(2)}) %collective-permute-start.6) | collective-permute-done | bytes 262176 | tf_op jit(solution)/shard_map/ppermute | solution.py:17
  101.9 0.7 copy-done.2
  102.6 0.9 pad_maximum_fusion.1
  103.4 1.3 collective-permute-start.7
  104.8 0.7 sub.43
  105.5 3.3 %all-to-all-start = ((s32[8,1,24]{2,1,0:T(1,128)}), s32[8,1,24]{2,1,0:T(1,128)S(1)}, u32[]{:S(2)}, u32[]{:S(2)}) async-start(s32[8,1,24]{2,1,0:T(1,128)} %sub.43), calls=%async_computation | async-start | bytes 8192 | tf_op jit(solution)/shard_map/all_to_all | solution.py:108
  108.8 7.7 %all-to-all-done = s32[8,1,24]{2,1,0:T(1,128)S(1)} async-done(((s32[8,1,24]{2,1,0:T(1,128)}), s32[8,1,24]{2,1,0:T(1,128)S(1)}, u32[]{:S(2)}, u32[]{:S(2)}) %all-to-all-start) | async-done | bytes 800 | tf_op jit(solution)/shard_map/all_to_all | solution.py:108
  116.5 0.5 broadcast.180
  117.1 0.6 reduce.3
  117.9 0.6 fusion.6
  118.6 2.2 %pad_maximum_fusion.refs_6_ = bf16[64,64,128]{2,1,0:T(8,128)(2,1)} fusion(bf16[32,64,128]{2,1,0:T(8,128)(2,1)} %collective-permute-done.7, bf16[16,64,128]{2,1,0:T(8,128)(2,1)} %copy-done.2, bf16[8,64,128]{2,1,0:T(8,128)(2,1)S(1)} %collective-permute-done.5, bf16[8,64,128]{2,1,0:T(8,128)(2,1)S(1)} %bitcast_bitcast_fusion), kind=kLoop, calls=%fused_computation.2 | loop fusion | flops 1572864 | bytes 2097152 | tf_op jit(solution)/shard_map/concatenate | solution.py:137
  120.8 16.7 %local_adjoint.1 = (f32[32,64,128]{2,1,0:T(8,128)}, bf16[32,64,128]{2,1,0:T(8,128)(2,1)}) custom-call(s32[192]{0:T(256)} %get-tuple-element.28.refs_0_, s32[192]{0:T(256)} %get-tuple-element.27.refs_1_, bf16[48,128,128]{2,1,0:T(8,128)(2,1)} %copy-done, bf16[48,128,128]{2,1,0:T(8,128)(2,1)} %copy-done.1, ...), custom_call_target="tpu_custom_call" | custom-call | tf_op jit(solution)/shard_map/local_adjoint/pallas_call | solution.py:144
  137.5 1.6 collective-permute-start.8
  139.1 10.6 %collective-permute-done.8 = bf16[32,64,128]{2,1,0:T(8,128)(2,1)S(1)} collective-permute-done((bf16[32,64,128]{2,1,0:T(8,128)(2,1)}, bf16[32,64,128]{2,1,0:T(8,128)(2,1)S(1)}, u32[]{:S(2)}, u32[]{:S(2)}) %collective-permute-start.8) | collective-permute-done | bytes 524320 | tf_op jit(solution)/shard_map/ppermute | solution.py:17
  149.7 1.4 convert_add_fusion
  151.2 0.9 collective-permute-start.9
  152.1 6.3 %collective-permute-done.9 = bf16[16,64,128]{2,1,0:T(8,128)(2,1)S(1)} collective-permute-done((bf16[16,64,128]{2,1,0:T(8,128)(2,1)S(1)}, bf16[16,64,128]{2,1,0:T(8,128)(2,1)S(1)}, u32[]{:S(2)}, u32[]{:S(2)}) %collective-permute-start.9) | collective-permute-done | bytes 262176 | tf_op jit(solution)/shard_map/ppermute | solution.py:17
  158.5 0.4 collective-permute-start.10
  158.9 6.9 %collective-permute-done.10 = bf16[8,64,128]{2,1,0:T(8,128)(2,1)S(1)} collective-permute-done((bf16[8,64,128]{2,1,0:T(8,128)(2,1)S(1)}, bf16[8,64,128]{2,1,0:T(8,128)(2,1)S(1)}, u32[]{:S(2)}, u32[]{:S(2)}) %collective-permute-start.10) | collective-permute-done | bytes 131104 | tf_op jit(solution)/shard_map/ppermute | solution.py:17
  165.8 0.7 copy_bitcast_fusion
  (36 shorter events, 1.2 us)
Async XLA Ops:
  4.7 45.7 %copy-start.3 = (bf16[64,1024]{1,0:T(8,128)(2,1)S(1)}, bf16[64,1024]{1,0:T(8,128)(2,1)}, u32[]{:S(2)}) copy-start(bf16[64,1024]{1,0:T(8,128)(2,1)} %param.11) | copy-start | bytes 393220
  48.9 71.9 %copy-start = (bf16[48,128,128]{2,1,0:T(8,128)(2,1)}, bf16[48,128,128]{2,1,0:T(8,128)(2,1)S(1)}, u32[]{:S(2)}) copy-start(bf16[48,128,128]{2,1,0:T(8,128)(2,1)S(1)} %all_to_all.11.refs_2_) | copy-start | bytes 4718596
  48.9 35.1 %collective-permute-start = (bf16[48,128,128]{2,1,0:T(8,128)(2,1)S(1)}, bf16[48,128,128]{2,1,0:T(8,128)(2,1)S(1)}, u32[]{:S(2)}, u32[]{:S(2)}) collective-permute-start(bf16[48,128,128]{2,1,0:T(8,128)(2,1)S(1)} %all_to_all.11.refs_2_), channel_id=1, source_target_pairs={{0,2},{1,3},{2,0},{3,1},{4,6},{5,7},{6,4},{7,5},{8,10},{9,11},{10,... | collective-permute-start | bytes 4718600 | tf_op jit(solution)/shard_map/ppermute | solution.py:17
  50.4 1.2 collective-permute-start.3
  51.7 32.2 %collective-permute-start.4 = (f32[1,1024]{1,0:T(1,128)S(1)}, f32[1,1024]{1,0:T(1,128)S(1)}, u32[]{:S(2)}, u32[]{:S(2)}) collective-permute-start(f32[1,1024]{1,0:T(1,128)S(1)} %add.108), channel_id=1, source_target_pairs={{0,2},{1,3},{2,0},{3,1},{4,6},{5,7},{6,4},{7,5},{8,10},{9,11},{10,... | collective-permute-start | bytes 12296 | tf_op jit(solution)/shard_map/ppermute | solution.py:17
  83.9 36.8 %collective-permute-start.1 = (bf16[48,128,128]{2,1,0:T(8,128)(2,1)S(1)}, bf16[48,128,128]{2,1,0:T(8,128)(2,1)}, u32[]{:S(2)}, u32[]{:S(2)}) collective-permute-start(bf16[48,128,128]{2,1,0:T(8,128)(2,1)S(1)} %all_to_all.11.refs_2_), channel_id=1, source_target_pairs={{0,1},{1,0},{2,3},{3,2},{4,5},{5,4},{6,7},{7,6},{8,9},{9,8},{10,11... | collective-permute-start | bytes 4718600 | tf_op jit(solution)/shard_map/ppermute | solution.py:17
  84.0 36.8 %copy-start.1 = (bf16[48,128,128]{2,1,0:T(8,128)(2,1)}, bf16[48,128,128]{2,1,0:T(8,128)(2,1)S(1)}, u32[]{:S(2)}) copy-start(bf16[48,128,128]{2,1,0:T(8,128)(2,1)S(1)} %collective-permute-done.refs_3_) | copy-start | bytes 4718596
  84.0 36.8 %collective-permute-start.2 = (bf16[48,128,128]{2,1,0:T(8,128)(2,1)S(1)}, bf16[48,128,128]{2,1,0:T(8,128)(2,1)}, u32[]{:S(2)}, u32[]{:S(2)}) collective-permute-start(bf16[48,128,128]{2,1,0:T(8,128)(2,1)S(1)} %collective-permute-done.refs_3_), channel_id=1, source_target_pairs={{0,1},{1,0},{2,3},{3,2},{4,5},{5,4},{6,7},{7,6},{8,9},{9,8},{10,11... | collective-permute-start | bytes 4718600 | tf_op jit(solution)/shard_map/ppermute | solution.py:17
  84.5 9.3 %collective-permute-start.5 = (bf16[8,64,128]{2,1,0:T(8,128)(2,1)S(1)}, bf16[8,64,128]{2,1,0:T(8,128)(2,1)S(1)}, u32[]{:S(2)}, u32[]{:S(2)}) collective-permute-start(bf16[8,64,128]{2,1,0:T(8,128)(2,1)S(1)} %bitcast_bitcast_fusion), channel_id=1, source_target_pairs={{0,16},{4,20},{8,24},{12,28},{16,0},{20,4},{24,8},{28,12},{1,17},{... | collective-permute-start | bytes 393224 | tf_op jit(solution)/shard_map/ppermute | solution.py:17
  93.8 8.0 %collective-permute-start.6 = (bf16[16,64,128]{2,1,0:T(8,128)(2,1)S(1)}, bf16[16,64,128]{2,1,0:T(8,128)(2,1)S(1)}, u32[]{:S(2)}, u32[]{:S(2)}) collective-permute-start(bf16[16,64,128]{2,1,0:T(8,128)(2,1)S(1)} %pad_maximum_fusion.2), channel_id=1, source_target_pairs={{0,8},{4,12},{8,0},{12,4},{16,24},{20,28},{24,16},{28,20},{1,9},{5... | collective-permute-start | bytes 786440 | tf_op jit(solution)/shard_map/ppermute | solution.py:17
  101.9 0.7 copy-start.2
  103.4 15.1 %collective-permute-start.7 = (bf16[32,64,128]{2,1,0:T(8,128)(2,1)}, bf16[32,64,128]{2,1,0:T(8,128)(2,1)}, u32[]{:S(2)}, u32[]{:S(2)}) collective-permute-start(bf16[32,64,128]{2,1,0:T(8,128)(2,1)} %pad_maximum_fusion.1), channel_id=1, source_target_pairs={{0,4},{4,0},{8,12},{12,8},{16,20},{20,16},{24,28},{28,24},{1,5},{5... | collective-permute-start | bytes 1572872 | tf_op jit(solution)/shard_map/ppermute | solution.py:17
  105.5 11.1 %all-to-all-start = ((s32[8,1,24]{2,1,0:T(1,128)}), s32[8,1,24]{2,1,0:T(1,128)S(1)}, u32[]{:S(2)}, u32[]{:S(2)}) async-start(s32[8,1,24]{2,1,0:T(1,128)} %sub.43), calls=%async_computation | async-start | bytes 8192 | tf_op jit(solution)/shard_map/all_to_all | solution.py:108
  137.5 12.2 %collective-permute-start.8 = (bf16[32,64,128]{2,1,0:T(8,128)(2,1)}, bf16[32,64,128]{2,1,0:T(8,128)(2,1)S(1)}, u32[]{:S(2)}, u32[]{:S(2)}) collective-permute-start(bf16[32,64,128]{2,1,0:T(8,128)(2,1)} %get-tuple-element.9), channel_id=1, source_target_pairs={{0,4},{4,0},{8,12},{12,8},{16,20},{20,16},{24,28},{28,24},{1,5},{5... | collective-permute-start | bytes 1572872 | tf_op jit(solution)/shard_map/ppermute | solution.py:17
  151.2 7.2 %collective-permute-start.9 = (bf16[16,64,128]{2,1,0:T(8,128)(2,1)S(1)}, bf16[16,64,128]{2,1,0:T(8,128)(2,1)S(1)}, u32[]{:S(2)}, u32[]{:S(2)}) collective-permute-start(bf16[16,64,128]{2,1,0:T(8,128)(2,1)S(1)} %slice.39), channel_id=1, source_target_pairs={{0,8},{4,12},{8,0},{12,4},{16,24},{20,28},{24,16},{28,20},{1,9},{5... | collective-permute-start | bytes 786440 | tf_op jit(solution)/shard_map/ppermute | solution.py:17
  158.5 7.3 %collective-permute-start.10 = (bf16[8,64,128]{2,1,0:T(8,128)(2,1)S(1)}, bf16[8,64,128]{2,1,0:T(8,128)(2,1)S(1)}, u32[]{:S(2)}, u32[]{:S(2)}) collective-permute-start(bf16[8,64,128]{2,1,0:T(8,128)(2,1)S(1)} %slice.40), channel_id=1, source_target_pairs={{0,16},{4,20},{8,24},{12,28},{16,0},{20,4},{24,8},{28,12},{1,17},{... | collective-permute-start | bytes 393224 | tf_op jit(solution)/shard_map/ppermute | solution.py:17

commit v2 on v1

v2 whole, which is shorter than its diff:
```python
import jax
import jax.numpy as jnp
from jax import lax
from jax.experimental import pallas as pl
from jax.experimental.pallas import tpu as pltpu
from jax.sharding import PartitionSpec as P

CHUNKS = 2


def rank_in_owner(owners):
    position = jnp.arange(owners.shape[0])
    earlier = (owners[:, None] == owners[None, :]) & (position[None, :] < position[:, None])
    return jnp.sum(earlier.astype(jnp.int32), axis=1)


def exchange(value, axis, distance):
    size = lax.axis_size(axis)
    return lax.ppermute(value, axis, [(i, i ^ distance) for i in range(size)])


def distances(size):
    found = []
    step = 1
    while step < size:
        found.append(step)
        step *= 2
    return found


def routes(size):
    first = distances(size)
    second = list(first)
    if len(second) > 1:
        second[0], second[1] = second[1], second[0]
    return first, second


def listed(relative, route):
    place = jnp.zeros_like(relative)
    for i, distance in enumerate(reversed(route)):
        place = place + (((relative // distance) & 1) << i)
    return place


def gather_pieces(value, route):
    pieces = [value]
    held = value
    for i, distance in enumerate(reversed(route)):
        pieces.append(exchange(held, "tile", distance))
        if i + 1 < len(route):
            held = jnp.concatenate([held, pieces[-1]], axis=0)
    return pieces


def load_flux(flux, pieces, piece_rows):
    cells, members, side = flux.shape
    half = cells // 2
    at = 0
    for refs, rows in zip(pieces, piece_rows):
        count = half // sum(ref.shape[0] // rows for ref in refs)
        for ref in refs:
            for l in range(ref.shape[0] // rows):
                flux[at : at + count] = ref[l * rows : l * rows + count * members].reshape(count, members, side)
                at += count


def run_forward(rows, cols, base, tiles, flux, modelled, unroll):
    cells = flux.shape[0]

    def step(i, carry):
        terms = []
        for u in range(unroll):
            t = i * unroll + u
            c = jnp.minimum(cols[base + t], cells - 1)
            terms.append(
                lax.dot_general(flux[c], tiles[t], (((1,), (1,)), ((), ())), preferred_element_type=jnp.float32)
            )
        for u in range(unroll):
            r = rows[base + i * unroll + u]
            modelled[r] = modelled[r] + terms[u]
        return carry

    lax.fori_loop(0, tiles.shape[0] // unroll, step, 0)


def run_backward(rows, cols, base, tiles, weighted, total, unroll):
    def step(i, carry):
        terms = []
        for u in range(unroll):
            t = i * unroll + u
            terms.append(jnp.dot(weighted[rows[base + t]], tiles[t], preferred_element_type=jnp.float32))
        for u in range(unroll):
            c = cols[base + i * unroll + u]
            total[c] = total[c] + terms[u]
        return carry

    lax.fori_loop(0, tiles.shape[0] // unroll, step, 0)


def forward_kernel(rows, cols, *refs, buffers, piece_rows, base, unroll):
    tiles, refs = refs[:buffers], refs[buffers:]
    count = (len(refs) - 2) // 2
    modelled, flux = refs[-2:]
    load_flux(flux, (refs[:count], refs[count : 2 * count]), piece_rows)
    modelled[...] = jnp.zeros_like(modelled)
    for b in range(buffers):
        run_forward(rows, cols, base + b * tiles[b].shape[0], tiles[b], flux, modelled, unroll)


def adjoint_kernel(rows, cols, *refs, buffers, new, carried, pieces, piece_rows, unroll):
    tiles, refs = refs[:buffers], refs[buffers:]
    groups, refs = (refs[:pieces], refs[pieces : 2 * pieces]), refs[2 * pieces :]
    if carried:
        earlier, refs = refs[0], refs[1:]
    observed, weight, near_a, far_a, near_b, far_b, modelled, weighted, total, flux = refs
    soundings = modelled.shape[0] - 1
    cells = flux.shape[0]
    side = flux.shape[2]
    per_buffer = tiles[0].shape[0]
    load_flux(flux, groups, piece_rows)
    if carried:
        modelled[...] = earlier[...]
    else:
        modelled[...] = jnp.zeros_like(modelled)
    total[...] = jnp.zeros_like(total)
    for b in range(buffers - new, buffers):
        run_forward(rows, cols, b * per_buffer, tiles[b], flux, modelled, unroll)
    scale = weight[...].astype(jnp.float32) / 8.0
    for r in range(soundings):
        part = slice(r * side, (r + 1) * side)
        weighted[r] = (scale[:, part] * (modelled[r] - observed[:, part])).astype(jnp.bfloat16)
    weighted[soundings] = jnp.zeros_like(weighted[soundings])
    for b in range(buffers):
        run_backward(rows, cols, b * per_buffer, tiles[b], weighted, total, unroll)
    quarter = cells // 4
    near_a[...] = total[:quarter]
    far_a[...] = total[quarter : 2 * quarter].astype(jnp.bfloat16)
    near_b[...] = total[2 * quarter : 3 * quarter]
    far_b[...] = total[3 * quarter : cells].astype(jnp.bfloat16)


def body(footprints, tile_row, tile_col, prior_flux, observed, precision_weight):
    devices_tile = lax.axis_size("tile")
    devices_mem = lax.axis_size("mem")
    me = lax.axis_index("tile")
    quarter = lax.axis_index("mem")
    tile_count, side, _ = footprints.shape
    local_members = prior_flux.shape[0]
    members = local_members * devices_mem
    flux_local = prior_flux.shape[1] // side
    half_local = flux_local // 2
    sound_local = observed.shape[1] // side
    flux_all = flux_local * devices_tile
    route_a, route_b = routes(devices_tile)

    capacity = tile_count // devices_tile + max(1, tile_count // (2 * devices_tile))
    share = -(-capacity // devices_mem)
    chunks = CHUNKS if share % CHUNKS == 0 else 1
    part = share // chunks
    capacity = share * devices_mem
    owner = tile_row // sound_local
    slot = owner * capacity + rank_in_owner(owner)
    wanted = (
        jnp.arange(devices_tile)[None, :, None] * capacity
        + quarter * share
        + jnp.arange(chunks)[:, None, None] * part
        + jnp.arange(part)[None, None, :]
    ).reshape(-1)
    hit = slot[None, :] == wanted[:, None]
    source = jnp.sum(jnp.where(hit, jnp.arange(tile_count)[None, :], 0), axis=1).reshape(chunks, -1)
    received = [
        lax.all_to_all(
            jnp.take(footprints, source[k], axis=0, mode="clip"), "tile", split_axis=0, concat_axis=0, tiled=True
        )
        for k in range(chunks)
    ]

    prior = prior_flux.astype(jnp.float32)
    mean = jnp.sum(prior, axis=0, keepdims=True)
    for distance in distances(devices_mem):
        mean = mean + exchange(mean, "mem", distance)
    anomalies = (prior - mean / members).astype(jnp.bfloat16)
    blocks = anomalies.reshape(local_members, flux_local, side).transpose(1, 0, 2).reshape(-1, side)

    digits = jnp.stack([tile_row % 128, tile_row // 128, tile_col % 128, tile_col // 128])
    digit_rows = -(-digits.size // side)
    digit_rows += -digit_rows % 16
    digits = jnp.pad(digits.reshape(-1), (0, digit_rows * side - digits.size)).reshape(digit_rows, side)
    half_rows = half_local * local_members
    rows_a = half_rows + digit_rows
    pieces_a = gather_pieces(
        jnp.concatenate([blocks[:half_rows], digits.astype(jnp.bfloat16)], axis=0), route_a
    )
    pieces_b = gather_pieces(blocks[half_rows:], route_b)

    listed_digits = jnp.concatenate(
        [p.reshape(-1, rows_a, side)[:, half_rows:] for p in pieces_a], axis=0
    ).reshape(devices_tile, -1)[:, : 4 * tile_count]
    places = listed(jnp.arange(devices_tile) ^ me, route_a)
    chosen = places[:, None] == jnp.arange(devices_tile)[None, :]
    ids = jnp.sum(jnp.where(chosen[:, :, None], listed_digits.astype(jnp.float32)[None], 0.0), axis=1)
    ids = ids.astype(jnp.int32).reshape(devices_tile, 4, tile_count)
    row = ids[:, 0] + 128 * ids[:, 1]
    col = ids[:, 2] + 128 * ids[:, 3]
    here = row // sound_local == me
    position = jnp.arange(tile_count)
    before = jnp.sum(
        (here[:, None, :] & (position[None, None, :] < position[None, :, None])).astype(jnp.int32), axis=2
    )
    relative = (col // flux_local) ^ me
    inner = col % flux_local
    upper = inner // half_local
    place = (
        upper * (flux_all // 2)
        + jnp.where(upper == 0, listed(relative, route_a), listed(relative, route_b)) * half_local
        + inner % half_local
    )
    code = (row % sound_local) * flux_all + place + 1
    order = [0]
    for distance in reversed(distances(devices_mem)):
        order = order + [q ^ distance for q in order]
    wanted = (
        (quarter ^ jnp.array(order))[None, :, None, None] * share
        + jnp.arange(chunks)[:, None, None, None] * part
        + jnp.arange(part)[None, None, None, :]
        + jnp.zeros((chunks, devices_mem, devices_tile, part), jnp.int32)
    )
    found = here[None, None, :, None, :] & (before[None, None, :, None, :] == wanted[..., None])
    table = jnp.sum(jnp.where(found, code[None, None, :, None, :], 0), axis=-1).reshape(-1) - 1
    rows = jnp.where(table >= 0, table // flux_all, sound_local)
    cols = jnp.where(table >= 0, table % flux_all, flux_all)

    buffers = []
    for k in range(chunks):
        held = [received[k]]
        for distance in reversed(distances(devices_mem)):
            held = held + [exchange(q, "mem", distance) for q in held]
        buffers.append(held)

    per_buffer = received[0].shape[0]
    unroll = 8
    while per_buffer % unroll:
        unroll //= 2
    vmem = pl.BlockSpec(memory_space=pltpu.VMEM)
    smem = pl.BlockSpec(memory_space=pltpu.SMEM)
    pieces = list(pieces_a) + list(pieces_b)
    piece_rows = (rows_a, half_rows)
    flux_scratch = pltpu.VMEM((flux_all, local_members, side), jnp.bfloat16)
    modelled_shape = (sound_local + 1, local_members, side)
    early = []
    if chunks > 1:
        old = [b for held in buffers[:-1] for b in held]
        early = [
            pl.pallas_call(
                lambda *refs: forward_kernel(
                    *refs, buffers=len(old), piece_rows=piece_rows, base=0, unroll=unroll
                ),
                out_shape=jax.ShapeDtypeStruct(modelled_shape, jnp.float32),
                in_specs=[smem, smem] + [vmem] * (len(old) + len(pieces)),
                out_specs=vmem,
                scratch_shapes=[flux_scratch],
                name="forward",
            )(rows, cols, *old, *pieces)
        ]
    tiles = [b for held in buffers for b in held]
    quarter_shape = (flux_all // 4, local_members, side)
    near_a, far_a, near_b, far_b = pl.pallas_call(
        lambda *refs: adjoint_kernel(
            *refs,
            buffers=len(tiles),
            new=devices_mem,
            carried=bool(early),
            pieces=len(pieces_a),
            piece_rows=piece_rows,
            unroll=unroll,
        ),
        out_shape=(
            jax.ShapeDtypeStruct(quarter_shape, jnp.float32),
            jax.ShapeDtypeStruct(quarter_shape, jnp.bfloat16),
        )
        * 2,
        in_specs=[smem, smem] + [vmem] * (len(tiles) + len(pieces) + len(early) + 2),
        out_specs=(vmem,) * 4,
        scratch_shapes=[
            pltpu.VMEM(modelled_shape, jnp.float32),
            pltpu.VMEM(modelled_shape, jnp.bfloat16),
            pltpu.VMEM((flux_all + 1, local_members, side), jnp.float32),
            flux_scratch,
        ],
        name="adjoint",
    )(rows, cols, *tiles, *pieces, *early, observed, precision_weight.reshape(1, -1))

    sums = []
    for near, far, route in ((near_a, far_a, route_a), (near_b, far_b, route_b)):
        for i, distance in enumerate(route):
            near = near + exchange(far, "tile", distance).astype(jnp.float32)
            if i + 1 < len(route):
                half = near.shape[0] // 2
                near, far = near[:half], near[half:].astype(jnp.bfloat16)
        sums.append(near)
    gradient = jnp.concatenate(sums, axis=0)
    return gradient.transpose(1, 0, 2).reshape(local_members, flux_local * side)


def solution(mesh):
    in_specs = (
        P("tile", None, None),
        P("tile"),
        P("tile"),
        P("mem", "tile"),
        P("mem", "tile"),
        P("tile"),
    )
    return jax.shard_map(body, mesh=mesh, in_specs=in_specs, out_specs=P("mem", "tile"), check_vma=False)
```

time: 167 us -> 150 us (0.90)
  blocking collectives: 44.2 us -> 0 us
  starting transfers between devices: 11.8 us -> 35.4 us
  waiting for transfers between devices: 80.1 us -> 72.5 us
  local copies, waits for them, and re-layouts: 5.51 us -> 10.9 us
  Pallas kernels: 16.7 us -> 19.9 us
  other arithmetic: 7.91 us -> 10.6 us
    all_to_all x1 -> x0, blocking collectives: 44.2 us -> none  [body(): got = lax.all_to_all(sent, 'tile', split_axis=0, concat_axis=0, tiled=True)]
    ppermute x11 -> x20, starting transfers between devices: 8.54 us -> 25.1 us  [exchange(): return lax.ppermute(value, axis, [(i, i ^ distance) for i in range(size)])]
    ppermute x11 -> x20, waiting for transfers between devices: 72.4 us -> 61 us  [exchange(): return lax.ppermute(value, axis, [(i, i ^ distance) for i in range(size)])]
    all_to_all x1 -> x2, starting transfers between devices: 3.26 us -> 10.4 us  [body(): lax.all_to_all(jnp.take(footprints, source[k], axis=0, mode='clip'), 'til...]
    gather x1 -> x2, local copies, waits for them, and re-layouts: 3.04 us -> 7.5 us  [body(): jnp.take(footprints, source[k], axis=0, mode='clip')]
    all_to_all x1 -> x2, waiting for transfers between devices: 7.74 us -> 11.5 us  [body(): lax.all_to_all(jnp.take(footprints, source[k], axis=0, mode='clip'), 'til...]
    pallas_call x1 -> x2, Pallas kernels: 16.7 us -> 19.9 us  [the longest x1 13.4 us: body(): pl.pallas_call(lambda *refs: adjoint_kernel(*refs, buffers=len(tiles), ne...]
    concatenate x3 -> x4, other arithmetic: 3.1 us -> 0.78 us  [gather_pieces(): held = jnp.concatenate([held, pieces[-1]], axis=0)]
  transfers between devices with their start and end apart: 12 -> 22, of which waited for: 8 -> 10; matrix products, arithmetic and copies ran while one was open for 4% -> 13% of each run, Pallas kernels for 0% -> 4%
where the time goes in v2:
time: 150 us
  waiting for transfers between devices  72.5 us (48%)
  starting transfers between devices  35.4 us (24%)
  Pallas kernels  19.9 us (13%)
  local copies, waits for them, and re-layouts  10.9 us (7%)
  other arithmetic  10.6 us (7%)
    ppermute x20, waiting for transfers between devices, exchange(): return lax.ppermute(value, axis, [(i, i ^ distance) for i in range(size)])  61 us
    ppermute x20, starting transfers between devices, exchange(): return lax.ppermute(value, axis, [(i, i ^ distance) for i in range(size)])  25.1 us
    pallas_call x1, Pallas kernels, body(): pl.pallas_call(lambda *refs: adjoint_kernel(*refs, buffers=len(tiles), ne...  13.4 us
    all_to_all x2, waiting for transfers between devices, body(): lax.all_to_all(jnp.take(footprints, source[k], axis=0, mode='clip'), 'til...  11.5 us
    all_to_all x2, starting transfers between devices, body(): lax.all_to_all(jnp.take(footprints, source[k], axis=0, mode='clip'), 'til...  10.4 us
    gather x2, local copies, waits for them, and re-layouts, body(): jnp.take(footprints, source[k], axis=0, mode='clip')  7.5 us
    pallas_call x1, Pallas kernels, body(): pl.pallas_call(lambda *refs: forward_kernel(*refs, buffers=len(old), piec...  6.51 us
  transfers between devices with their start and end apart: 22, of which 10 were waited for; matrix products, arithmetic and copies ran while one was open for 13% of the time, Pallas kernels for 4%

profile of v2, /device:TPU:0, one launch (start us, length us, event | category | flops | bytes accessed | tf_op | source)
XLA Modules:
  0.0 149.8 jit_solution(10511418581577142280)
XLA Ops:
  0.0 0.9 convert_reduce_fusion.1
  2.9 3.8 %gather_fusion.1 = bf16[24,128,128]{2,1,0:T(8,128)(2,1)} fusion(bf16[128,128,128]{2,1,0:T(8,128)(2,1)} %param.7, s32[1024]{0:T(1024)S(1)} %pad_clamp_fusion), kind=kCustom, calls=%fused_computation.1 | custom fusion | bytes 1572960 | tf_op jit(solution)/shard_map/jit(_take)/gather | solution.py:174
  6.6 6.8 %all-to-all-start.1 = ((bf16[24,128,128]{2,1,0:T(8,128)(2,1)}), bf16[24,128,128]{2,1,0:T(8,128)(2,1)S(1)}, u32[]{:S(2)}, u32[]{:S(2)}) async-start(bf16[24,128,128]{2,1,0:T(8,128)(2,1)} %gather_fusion.1), calls=%async_computation.1 | async-start | bytes 1572864 | tf_op jit(solution)/shard_map/all_to_all | solution.py:173
  14.9 1.6 %collective-permute-start.1 = (f32[1,1024]{1,0:T(1,128)S(1)}, f32[1,1024]{1,0:T(1,128)S(1)}, u32[]{:S(2)}, u32[]{:S(2)}) collective-permute-start(f32[1,1024]{1,0:T(1,128)S(1)} %add.301), channel_id=1, source_target_pairs={{0,2},{1,3},{2,0},{3,1},{4,6},{5,7},{6,4},{7,5},{8,10},{9,11},{10,... | collective-permute-start | bytes 12296 | tf_op jit(solution)/shard_map/ppermute | solution.py:19
  16.5 2.1 %collective-permute-done.1 = f32[1,1024]{1,0:T(1,128)S(1)} collective-permute-done((f32[1,1024]{1,0:T(1,128)S(1)}, f32[1,1024]{1,0:T(1,128)S(1)}, u32[]{:S(2)}, u32[]{:S(2)}) %collective-permute-start.1) | collective-permute-done | bytes 4128 | tf_op jit(solution)/shard_map/ppermute | solution.py:19
  18.6 0.9 bitcast_bitcast_fusion
  19.6 3.0 %collective-permute-start.2 = (bf16[272,128]{1,0:T(8,128)(2,1)S(1)}, bf16[272,128]{1,0:T(8,128)(2,1)S(1)}, u32[]{:S(2)}, u32[]{:S(2)}) collective-permute-start(bf16[272,128]{1,0:T(8,128)(2,1)S(1)} %get-tuple-element.16.refs_6_.refs_10_), channel_id=1, source_target_pairs={{0,16},{4,20},{8,24},{12,28},{16,0},{20,4},{24,8},{28,12},{1,17},{... | collective-permute-start | bytes 208904 | tf_op jit(solution)/shard_map/ppermute | solution.py:19
  22.6 3.8 %gather_fusion = bf16[24,128,128]{2,1,0:T(8,128)(2,1)} fusion(bf16[128,128,128]{2,1,0:T(8,128)(2,1)} %param.7, s32[1024]{0:T(1024)S(1)} %pad_clamp_fusion.1), kind=kCustom, calls=%fused_computation | custom fusion | bytes 1572960 | tf_op jit(solution)/shard_map/jit(_take)/gather | solution.py:174
  26.4 11.5 %all-to-all-done.1.refs_6_ = bf16[24,128,128]{2,1,0:T(8,128)(2,1)S(1)} async-done(((bf16[24,128,128]{2,1,0:T(8,128)(2,1)}), bf16[24,128,128]{2,1,0:T(8,128)(2,1)S(1)}, u32[]{:S(2)}, u32[]{:S(2)}) %all-to-all-start.1) | async-done | bytes 786464 | tf_op jit(solution)/shard_map/all_to_all | solution.py:173
  37.9 3.5 %all-to-all-start = ((bf16[24,128,128]{2,1,0:T(8,128)(2,1)}), bf16[24,128,128]{2,1,0:T(8,128)(2,1)S(1)}, u32[]{:S(2)}, u32[]{:S(2)}) async-start(bf16[24,128,128]{2,1,0:T(8,128)(2,1)} %gather_fusion), calls=%async_computation | async-start | bytes 1572864 | tf_op jit(solution)/shard_map/all_to_all | solution.py:173
  41.5 2.0 %collective-permute-start.3 = (bf16[544,128]{1,0:T(8,128)(2,1)S(1)}, bf16[544,128]{1,0:T(8,128)(2,1)S(1)}, u32[]{:S(2)}, u32[]{:S(2)}) collective-permute-start(bf16[544,128]{1,0:T(8,128)(2,1)S(1)} %pad_maximum_fusion.2), channel_id=1, source_target_pairs={{0,8},{4,12},{8,0},{12,4},{16,24},{20,28},{24,16},{28,20},{1,9},{5... | collective-permute-start | bytes 417800 | tf_op jit(solution)/shard_map/ppermute | solution.py:19
  43.5 1.5 %collective-permute-start.12 = (bf16[512,128]{1,0:T(8,128)(2,1)S(1)}, bf16[512,128]{1,0:T(8,128)(2,1)S(1)}, u32[]{:S(2)}, u32[]{:S(2)}) collective-permute-start(bf16[512,128]{1,0:T(8,128)(2,1)S(1)} %pad_maximum_fusion.3), channel_id=1, source_target_pairs={{0,4},{4,0},{8,12},{12,8},{16,20},{20,16},{24,28},{28,24},{1,5},{5... | collective-permute-start | bytes 393224 | tf_op jit(solution)/shard_map/ppermute | solution.py:19
  45.1 11.7 %collective-permute-done.3.refs_8_.refs_12_ = bf16[544,128]{1,0:T(8,128)(2,1)S(1)} collective-permute-done((bf16[544,128]{1,0:T(8,128)(2,1)S(1)}, bf16[544,128]{1,0:T(8,128)(2,1)S(1)}, u32[]{:S(2)}, u32[]{:S(2)}) %collective-permute-start.3) | collective-permute-done | bytes 139296 | tf_op jit(solution)/shard_map/ppermute | solution.py:19
  56.8 1.9 %collective-permute-start.4 = (bf16[1088,128]{1,0:T(8,128)(2,1)S(1)}, bf16[1088,128]{1,0:T(8,128)(2,1)S(1)}, u32[]{:S(2)}, u32[]{:S(2)}) collective-permute-start(bf16[1088,128]{1,0:T(8,128)(2,1)S(1)} %pad_maximum_fusion), channel_id=1, source_target_pairs={{0,4},{4,0},{8,12},{12,8},{16,20},{20,16},{24,28},{28,24},{1,5},{5... | collective-permute-start | bytes 835592 | tf_op jit(solution)/shard_map/ppermute | solution.py:19
  59.5 2.5 %collective-permute-start.13 = (bf16[1024,128]{1,0:T(8,128)(2,1)}, bf16[1024,128]{1,0:T(8,128)(2,1)}, u32[]{:S(2)}, u32[]{:S(2)}) collective-permute-start(bf16[1024,128]{1,0:T(8,128)(2,1)} %pad_maximum_fusion.1), channel_id=1, source_target_pairs={{0,8},{4,12},{8,0},{12,4},{16,24},{20,28},{24,16},{28,20},{1,9},{5... | collective-permute-start | bytes 786440 | tf_op jit(solution)/shard_map/ppermute | solution.py:19
  62.0 2.2 %collective-permute-done.4.refs_9_.refs_13_ = bf16[1088,128]{1,0:T(8,128)(2,1)S(1)} collective-permute-done((bf16[1088,128]{1,0:T(8,128)(2,1)S(1)}, bf16[1088,128]{1,0:T(8,128)(2,1)S(1)}, u32[]{:S(2)}, u32[]{:S(2)}) %collective-permute-start.4) | collective-permute-done | bytes 278560 | tf_op jit(solution)/shard_map/ppermute | solution.py:19
  64.4 1.6 %collective-permute-start.8 = (bf16[24,128,128]{2,1,0:T(8,128)(2,1)S(1)}, bf16[24,128,128]{2,1,0:T(8,128)(2,1)}, u32[]{:S(2)}, u32[]{:S(2)}) collective-permute-start(bf16[24,128,128]{2,1,0:T(8,128)(2,1)S(1)} %all-to-all-done.1.refs_6_), channel_id=1, source_target_pairs={{0,2},{1,3},{2,0},{3,1},{4,6},{5,7},{6,4},{7,5},{8,10},{9,11},{10,... | collective-permute-start | bytes 2359304 | tf_op jit(solution)/shard_map/ppermute | solution.py:19
  67.4 17.6 %collective-permute-done.8.refs_7_ = bf16[24,128,128]{2,1,0:T(8,128)(2,1)} collective-permute-done((bf16[24,128,128]{2,1,0:T(8,128)(2,1)S(1)}, bf16[24,128,128]{2,1,0:T(8,128)(2,1)}, u32[]{:S(2)}, u32[]{:S(2)}) %collective-permute-start.8) | collective-permute-done | bytes 786464 | tf_op jit(solution)/shard_map/ppermute | solution.py:19
  85.0 14.0 %collective-permute-done.5.refs_3_ = bf16[24,128,128]{2,1,0:T(8,128)(2,1)S(1)} collective-permute-done((bf16[24,128,128]{2,1,0:T(8,128)(2,1)S(1)}, bf16[24,128,128]{2,1,0:T(8,128)(2,1)S(1)}, u32[]{:S(2)}, u32[]{:S(2)}) %collective-permute-start.5) | collective-permute-done | bytes 786464 | tf_op jit(solution)/shard_map/ppermute | solution.py:19
  100.2 1.4 copy.16
  104.0 6.5 %forward.1.refs_18_ = f32[17,64,128]{2,1,0:T(8,128)} custom-call(s32[192]{0:T(256)} %get-tuple-element.18.refs_0_, s32[192]{0:T(256)} %get-tuple-element.17.refs_1_, bf16[24,128,128]{2,1,0:T(8,128)(2,1)} %copy-done, bf16[24,128,128]{2,1,0:T(8,128)(2,1)} %copy-done.2, bf16[24,128,128]{2,1,0:T(8,128)(2,1)} %copy-done.3, ...), custom_call_target="tpu_custom_call" | custom-call | tf_op jit(solution)/shard_map/forward/pallas_call | solution.py:255
  110.6 13.4 %adjoint.1 = (f32[16,64,128]{2,1,0:T(8,128)}, bf16[16,64,128]{2,1,0:T(8,128)(2,1)}, f32[16,64,128]{2,1,0:T(8,128)}, bf16[16,64,128]{2,1,0:T(8,128)(2,1)}) custom-call(s32[192]{0:T(256)} %get-tuple-element.18.refs_0_, s32[192]{0:T(256)} %get-tuple-element.17.refs_1_, bf16[24,128,128]{2,1,0:T(8,128)(2,1)} %copy-done, bf16[24,128,128]{2,1,0:T(8,128)(2,1)} %copy-done.2, ...), custom_call_target="tpu_custom_call" | custom-call | tf_op jit(solution)/shard_map/adjoint/pallas_call | solution.py:268
  123.9 2.6 %collective-permute-start.14 = (bf16[16,64,128]{2,1,0:T(8,128)(2,1)}, bf16[16,64,128]{2,1,0:T(8,128)(2,1)S(1)}, u32[]{:S(2)}, u32[]{:S(2)}) collective-permute-start(bf16[16,64,128]{2,1,0:T(8,128)(2,1)} %get-tuple-element.10), channel_id=1, source_target_pairs={{0,4},{4,0},{8,12},{12,8},{16,20},{20,16},{24,28},{28,24},{1,5},{5... | collective-permute-start | bytes 786440 | tf_op jit(solution)/shard_map/ppermute | solution.py:19
  127.0 6.6 %collective-permute-done.14 = bf16[16,64,128]{2,1,0:T(8,128)(2,1)S(1)} collective-permute-done((bf16[16,64,128]{2,1,0:T(8,128)(2,1)}, bf16[16,64,128]{2,1,0:T(8,128)(2,1)S(1)}, u32[]{:S(2)}, u32[]{:S(2)}) %collective-permute-start.14) | collective-permute-done | bytes 262176 | tf_op jit(solution)/shard_map/ppermute | solution.py:19
  133.7 1.1 convert_add_fusion.1
  134.8 1.5 %collective-permute-start.15 = (bf16[8,64,128]{2,1,0:T(8,128)(2,1)S(1)}, bf16[8,64,128]{2,1,0:T(8,128)(2,1)S(1)}, u32[]{:S(2)}, u32[]{:S(2)}) collective-permute-start(bf16[8,64,128]{2,1,0:T(8,128)(2,1)S(1)} %slice.157), channel_id=1, source_target_pairs={{0,8},{4,12},{8,0},{12,4},{16,24},{20,28},{24,16},{28,20},{1,9},{5... | collective-permute-start | bytes 393224 | tf_op jit(solution)/shard_map/ppermute | solution.py:19
  136.4 1.1 convert_add_fusion
  138.4 1.9 %collective-permute-done.15 = bf16[8,64,128]{2,1,0:T(8,128)(2,1)S(1)} collective-permute-done((bf16[8,64,128]{2,1,0:T(8,128)(2,1)S(1)}, bf16[8,64,128]{2,1,0:T(8,128)(2,1)S(1)}, u32[]{:S(2)}, u32[]{:S(2)}) %collective-permute-start.15) | collective-permute-done | bytes 131104 | tf_op jit(solution)/shard_map/ppermute | solution.py:19
  140.3 2.7 %collective-permute-start.16 = (bf16[4,64,128]{2,1,0:T(8,128)(2,1)S(1)}, bf16[4,64,128]{2,1,0:T(8,128)(2,1)S(1)}, u32[]{:S(2)}, u32[]{:S(2)}) collective-permute-start(bf16[4,64,128]{2,1,0:T(8,128)(2,1)S(1)} %slice.159), channel_id=1, source_target_pairs={{0,16},{4,20},{8,24},{12,28},{16,0},{20,4},{24,8},{28,12},{1,17},{... | collective-permute-start | bytes 196616 | tf_op jit(solution)/shard_map/ppermute | solution.py:19
  143.0 1.2 collective-permute-start.19
  144.2 3.9 %collective-permute-done.16 = bf16[4,64,128]{2,1,0:T(8,128)(2,1)S(1)} collective-permute-done((bf16[4,64,128]{2,1,0:T(8,128)(2,1)S(1)}, bf16[4,64,128]{2,1,0:T(8,128)(2,1)S(1)}, u32[]{:S(2)}, u32[]{:S(2)}) %collective-permute-start.16) | collective-permute-done | bytes 65568 | tf_op jit(solution)/shard_map/ppermute | solution.py:19
  148.1 0.9 collective-permute-done.19
  (98 shorter events, 11.8 us)
Async XLA Ops:
  0.9 14.0 %collective-permute-start = (f32[1,1024]{1,0:T(1,128)S(1)}, f32[1,1024]{1,0:T(1,128)S(1)}, u32[]{:S(2)}, u32[]{:S(2)}) collective-permute-start(f32[1,1024]{1,0:T(1,128)S(1)} %bitcast.89), channel_id=1, source_target_pairs={{0,1},{1,0},{2,3},{3,2},{4,5},{5,4},{6,7},{7,6},{8,9},{9,8},{10,11... | collective-permute-start | bytes 12296 | tf_op jit(solution)/shard_map/ppermute | solution.py:19
  6.6 31.3 %all-to-all-start.1 = ((bf16[24,128,128]{2,1,0:T(8,128)(2,1)}), bf16[24,128,128]{2,1,0:T(8,128)(2,1)S(1)}, u32[]{:S(2)}, u32[]{:S(2)}) async-start(bf16[24,128,128]{2,1,0:T(8,128)(2,1)} %gather_fusion.1), calls=%async_computation.1 | async-start | bytes 1572864 | tf_op jit(solution)/shard_map/all_to_all | solution.py:173
  14.9 3.7 %collective-permute-start.1 = (f32[1,1024]{1,0:T(1,128)S(1)}, f32[1,1024]{1,0:T(1,128)S(1)}, u32[]{:S(2)}, u32[]{:S(2)}) collective-permute-start(f32[1,1024]{1,0:T(1,128)S(1)} %add.301), channel_id=1, source_target_pairs={{0,2},{1,3},{2,0},{3,1},{4,6},{5,7},{6,4},{7,5},{8,10},{9,11},{10,... | collective-permute-start | bytes 12296 | tf_op jit(solution)/shard_map/ppermute | solution.py:19
  19.6 83.6 %copy-start.4 = (bf16[4,64,128]{2,1,0:T(8,128)(2,1)}, bf16[4,64,128]{2,1,0:T(8,128)(2,1)S(1)}, u32[]{:S(2)}) copy-start(bf16[4,64,128]{2,1,0:T(8,128)(2,1)S(1)} %get-tuple-element.13) | copy-start | bytes 196612
  19.6 37.2 %copy-start.10 = (bf16[272,128]{1,0:T(8,128)(2,1)}, bf16[272,128]{1,0:T(8,128)(2,1)S(1)}, u32[]{:S(2)}) copy-start(bf16[272,128]{1,0:T(8,128)(2,1)S(1)} %get-tuple-element.16.refs_6_.refs_10_) | copy-start | bytes 208900
  19.6 21.8 %collective-permute-start.2 = (bf16[272,128]{1,0:T(8,128)(2,1)S(1)}, bf16[272,128]{1,0:T(8,128)(2,1)S(1)}, u32[]{:S(2)}, u32[]{:S(2)}) collective-permute-start(bf16[272,128]{1,0:T(8,128)(2,1)S(1)} %get-tuple-element.16.refs_6_.refs_10_), channel_id=1, source_target_pairs={{0,16},{4,20},{8,24},{12,28},{16,0},{20,4},{24,8},{28,12},{1,17},{... | collective-permute-start | bytes 208904 | tf_op jit(solution)/shard_map/ppermute | solution.py:19
  26.4 17.1 %collective-permute-start.11 = (bf16[256,128]{1,0:T(8,128)(2,1)S(1)}, bf16[256,128]{1,0:T(8,128)(2,1)S(1)}, u32[]{:S(2)}, u32[]{:S(2)}) collective-permute-start(bf16[256,128]{1,0:T(8,128)(2,1)S(1)} %bitcast.76), channel_id=1, source_target_pairs={{0,16},{4,20},{8,24},{12,28},{16,0},{20,4},{24,8},{28,12},{1,17},{... | collective-permute-start | bytes 196616 | tf_op jit(solution)/shard_map/ppermute | solution.py:19
  37.9 72.6 %copy-start.1 = (bf16[24,128,128]{2,1,0:T(8,128)(2,1)}, bf16[24,128,128]{2,1,0:T(8,128)(2,1)S(1)}, u32[]{:S(2)}) copy-start(bf16[24,128,128]{2,1,0:T(8,128)(2,1)S(1)} %all-to-all-done.1.refs_6_) | copy-start | bytes 2359300
  37.9 28.1 %all-to-all-start = ((bf16[24,128,128]{2,1,0:T(8,128)(2,1)}), bf16[24,128,128]{2,1,0:T(8,128)(2,1)S(1)}, u32[]{:S(2)}, u32[]{:S(2)}) async-start(bf16[24,128,128]{2,1,0:T(8,128)(2,1)} %gather_fusion), calls=%async_computation | async-start | bytes 1572864 | tf_op jit(solution)/shard_map/all_to_all | solution.py:173
  41.5 61.7 %copy-start.8 = (bf16[272,128]{1,0:T(8,128)(2,1)}, bf16[272,128]{1,0:T(8,128)(2,1)S(1)}, u32[]{:S(2)}) copy-start(bf16[272,128]{1,0:T(8,128)(2,1)S(1)} %collective-permute-done.2.refs_7_.refs_11_) | copy-start | bytes 208900
  41.5 15.3 %collective-permute-start.3 = (bf16[544,128]{1,0:T(8,128)(2,1)S(1)}, bf16[544,128]{1,0:T(8,128)(2,1)S(1)}, u32[]{:S(2)}, u32[]{:S(2)}) collective-permute-start(bf16[544,128]{1,0:T(8,128)(2,1)S(1)} %pad_maximum_fusion.2), channel_id=1, source_target_pairs={{0,8},{4,12},{8,0},{12,4},{16,24},{20,28},{24,16},{28,20},{1,9},{5... | collective-permute-start | bytes 417800 | tf_op jit(solution)/shard_map/ppermute | solution.py:19
  43.5 22.5 %copy-start.9 = (bf16[256,128]{1,0:T(8,128)(2,1)}, bf16[256,128]{1,0:T(8,128)(2,1)S(1)}, u32[]{:S(2)}) copy-start(bf16[256,128]{1,0:T(8,128)(2,1)S(1)} %collective-permute-done.11.refs_11_.refs_15_) | copy-start | bytes 196612
  43.5 15.3 %collective-permute-start.12 = (bf16[512,128]{1,0:T(8,128)(2,1)S(1)}, bf16[512,128]{1,0:T(8,128)(2,1)S(1)}, u32[]{:S(2)}, u32[]{:S(2)}) collective-permute-start(bf16[512,128]{1,0:T(8,128)(2,1)S(1)} %pad_maximum_fusion.3), channel_id=1, source_target_pairs={{0,4},{4,0},{8,12},{12,8},{16,20},{20,16},{24,28},{28,24},{1,5},{5... | collective-permute-start | bytes 393224 | tf_op jit(solution)/shard_map/ppermute | solution.py:19
  56.8 46.4 %copy-start.5 = (bf16[544,128]{1,0:T(8,128)(2,1)}, bf16[544,128]{1,0:T(8,128)(2,1)S(1)}, u32[]{:S(2)}) copy-start(bf16[544,128]{1,0:T(8,128)(2,1)S(1)} %collective-permute-done.3.refs_8_.refs_12_) | copy-start | bytes 417796
  56.8 7.4 %collective-permute-start.4 = (bf16[1088,128]{1,0:T(8,128)(2,1)S(1)}, bf16[1088,128]{1,0:T(8,128)(2,1)S(1)}, u32[]{:S(2)}, u32[]{:S(2)}) collective-permute-start(bf16[1088,128]{1,0:T(8,128)(2,1)S(1)} %pad_maximum_fusion), channel_id=1, source_target_pairs={{0,4},{4,0},{8,12},{12,8},{16,20},{20,16},{24,28},{28,24},{1,5},{5... | collective-permute-start | bytes 835592 | tf_op jit(solution)/shard_map/ppermute | solution.py:19
  58.8 44.4 %copy-start.7 = (bf16[512,128]{1,0:T(8,128)(2,1)}, bf16[512,128]{1,0:T(8,128)(2,1)S(1)}, u32[]{:S(2)}) copy-start(bf16[512,128]{1,0:T(8,128)(2,1)S(1)} %collective-permute-done.12.refs_12_.refs_16_) | copy-start | bytes 393220
  59.5 43.6 %collective-permute-start.13 = (bf16[1024,128]{1,0:T(8,128)(2,1)}, bf16[1024,128]{1,0:T(8,128)(2,1)}, u32[]{:S(2)}, u32[]{:S(2)}) collective-permute-start(bf16[1024,128]{1,0:T(8,128)(2,1)} %pad_maximum_fusion.1), channel_id=1, source_target_pairs={{0,8},{4,12},{8,0},{12,4},{16,24},{20,28},{24,16},{28,20},{1,9},{5... | collective-permute-start | bytes 786440 | tf_op jit(solution)/shard_map/ppermute | solution.py:19
  64.2 1.7 %copy-start.6 = (bf16[1088,128]{1,0:T(8,128)(2,1)}, bf16[1088,128]{1,0:T(8,128)(2,1)S(1)}, u32[]{:S(2)}) copy-start(bf16[1088,128]{1,0:T(8,128)(2,1)S(1)} %collective-permute-done.4.refs_9_.refs_13_) | copy-start | bytes 835588
  64.4 20.6 %collective-permute-start.8 = (bf16[24,128,128]{2,1,0:T(8,128)(2,1)S(1)}, bf16[24,128,128]{2,1,0:T(8,128)(2,1)}, u32[]{:S(2)}, u32[]{:S(2)}) collective-permute-start(bf16[24,128,128]{2,1,0:T(8,128)(2,1)S(1)} %all-to-all-done.1.refs_6_), channel_id=1, source_target_pairs={{0,2},{1,3},{2,0},{3,1},{4,6},{5,7},{6,4},{7,5},{8,10},{9,11},{10,... | collective-permute-start | bytes 2359304 | tf_op jit(solution)/shard_map/ppermute | solution.py:19
  66.0 37.2 %copy-start = (bf16[24,128,128]{2,1,0:T(8,128)(2,1)}, bf16[24,128,128]{2,1,0:T(8,128)(2,1)S(1)}, u32[]{:S(2)}) copy-start(bf16[24,128,128]{2,1,0:T(8,128)(2,1)S(1)} %all-to-all-done.refs_2_) | copy-start | bytes 2359300
  66.0 33.0 %collective-permute-start.5 = (bf16[24,128,128]{2,1,0:T(8,128)(2,1)S(1)}, bf16[24,128,128]{2,1,0:T(8,128)(2,1)S(1)}, u32[]{:S(2)}, u32[]{:S(2)}) collective-permute-start(bf16[24,128,128]{2,1,0:T(8,128)(2,1)S(1)} %all-to-all-done.refs_2_), channel_id=1, source_target_pairs={{0,2},{1,3},{2,0},{3,1},{4,6},{5,7},{6,4},{7,5},{8,10},{9,11},{10,... | collective-permute-start | bytes 2359304 | tf_op jit(solution)/shard_map/ppermute | solution.py:19
  66.8 43.7 %collective-permute-start.9 = (bf16[24,128,128]{2,1,0:T(8,128)(2,1)S(1)}, bf16[24,128,128]{2,1,0:T(8,128)(2,1)}, u32[]{:S(2)}, u32[]{:S(2)}) collective-permute-start(bf16[24,128,128]{2,1,0:T(8,128)(2,1)S(1)} %all-to-all-done.1.refs_6_), channel_id=1, source_target_pairs={{0,1},{1,0},{2,3},{3,2},{4,5},{5,4},{6,7},{7,6},{8,9},{9,8},{10,11... | collective-permute-start | bytes 2359304 | tf_op jit(solution)/shard_map/ppermute | solution.py:19
  66.9 36.2 %collective-permute-start.6 = (bf16[24,128,128]{2,1,0:T(8,128)(2,1)S(1)}, bf16[24,128,128]{2,1,0:T(8,128)(2,1)S(1)}, u32[]{:S(2)}, u32[]{:S(2)}) collective-permute-start(bf16[24,128,128]{2,1,0:T(8,128)(2,1)S(1)} %all-to-all-done.refs_2_), channel_id=1, source_target_pairs={{0,1},{1,0},{2,3},{3,2},{4,5},{5,4},{6,7},{7,6},{8,9},{9,8},{10,11... | collective-permute-start | bytes 2359304 | tf_op jit(solution)/shard_map/ppermute | solution.py:19
  85.0 25.6 %collective-permute-start.10 = (bf16[24,128,128]{2,1,0:T(8,128)(2,1)}, bf16[24,128,128]{2,1,0:T(8,128)(2,1)}, u32[]{:S(2)}, u32[]{:S(2)}) collective-permute-start(bf16[24,128,128]{2,1,0:T(8,128)(2,1)} %collective-permute-done.8.refs_7_), channel_id=1, source_target_pairs={{0,1},{1,0},{2,3},{3,2},{4,5},{5,4},{6,7},{7,6},{8,9},{9,8},{10,11... | collective-permute-start | bytes 2359304 | tf_op jit(solution)/shard_map/ppermute | solution.py:19
  99.0 4.2 %copy-start.2 = (bf16[24,128,128]{2,1,0:T(8,128)(2,1)}, bf16[24,128,128]{2,1,0:T(8,128)(2,1)S(1)}, u32[]{:S(2)}) copy-start(bf16[24,128,128]{2,1,0:T(8,128)(2,1)S(1)} %collective-permute-done.5.refs_3_) | copy-start | bytes 2359300
  99.0 4.1 %collective-permute-start.7 = (bf16[24,128,128]{2,1,0:T(8,128)(2,1)S(1)}, bf16[24,128,128]{2,1,0:T(8,128)(2,1)}, u32[]{:S(2)}, u32[]{:S(2)}) collective-permute-start(bf16[24,128,128]{2,1,0:T(8,128)(2,1)S(1)} %collective-permute-done.5.refs_3_), channel_id=1, source_target_pairs={{0,1},{1,0},{2,3},{3,2},{4,5},{5,4},{6,7},{7,6},{8,9},{9,8},{10,11... | collective-permute-start | bytes 2359304 | tf_op jit(solution)/shard_map/ppermute | solution.py:19
  123.9 9.7 %collective-permute-start.14 = (bf16[16,64,128]{2,1,0:T(8,128)(2,1)}, bf16[16,64,128]{2,1,0:T(8,128)(2,1)S(1)}, u32[]{:S(2)}, u32[]{:S(2)}) collective-permute-start(bf16[16,64,128]{2,1,0:T(8,128)(2,1)} %get-tuple-element.10), channel_id=1, source_target_pairs={{0,4},{4,0},{8,12},{12,8},{16,20},{20,16},{24,28},{28,24},{1,5},{5... | collective-permute-start | bytes 786440 | tf_op jit(solution)/shard_map/ppermute | solution.py:19
  126.5 9.9 %collective-permute-start.17 = (bf16[16,64,128]{2,1,0:T(8,128)(2,1)}, bf16[16,64,128]{2,1,0:T(8,128)(2,1)S(1)}, u32[]{:S(2)}, u32[]{:S(2)}) collective-permute-start(bf16[16,64,128]{2,1,0:T(8,128)(2,1)} %get-tuple-element.12), channel_id=1, source_target_pairs={{0,8},{4,12},{8,0},{12,4},{16,24},{20,28},{24,16},{28,20},{1,9},{5... | collective-permute-start | bytes 786440 | tf_op jit(solution)/shard_map/ppermute | solution.py:19
  134.8 5.4 %collective-permute-start.15 = (bf16[8,64,128]{2,1,0:T(8,128)(2,1)S(1)}, bf16[8,64,128]{2,1,0:T(8,128)(2,1)S(1)}, u32[]{:S(2)}, u32[]{:S(2)}) collective-permute-start(bf16[8,64,128]{2,1,0:T(8,128)(2,1)S(1)} %slice.157), channel_id=1, source_target_pairs={{0,8},{4,12},{8,0},{12,4},{16,24},{20,28},{24,16},{28,20},{1,9},{5... | collective-permute-start | bytes 393224 | tf_op jit(solution)/shard_map/ppermute | solution.py:19
  137.5 5.4 %collective-permute-start.18 = (bf16[8,64,128]{2,1,0:T(8,128)(2,1)S(1)}, bf16[8,64,128]{2,1,0:T(8,128)(2,1)S(1)}, u32[]{:S(2)}, u32[]{:S(2)}) collective-permute-start(bf16[8,64,128]{2,1,0:T(8,128)(2,1)S(1)} %slice.156), channel_id=1, source_target_pairs={{0,4},{4,0},{8,12},{12,8},{16,20},{20,16},{24,28},{28,24},{1,5},{5... | collective-permute-start | bytes 393224 | tf_op jit(solution)/shard_map/ppermute | solution.py:19
  140.3 7.8 %collective-permute-start.16 = (bf16[4,64,128]{2,1,0:T(8,128)(2,1)S(1)}, bf16[4,64,128]{2,1,0:T(8,128)(2,1)S(1)}, u32[]{:S(2)}, u32[]{:S(2)}) collective-permute-start(bf16[4,64,128]{2,1,0:T(8,128)(2,1)S(1)} %slice.159), channel_id=1, source_target_pairs={{0,16},{4,20},{8,24},{12,28},{16,0},{20,4},{24,8},{28,12},{1,17},{... | collective-permute-start | bytes 196616 | tf_op jit(solution)/shard_map/ppermute | solution.py:19
  143.0 6.0 %collective-permute-start.19 = (bf16[4,64,128]{2,1,0:T(8,128)(2,1)S(1)}, bf16[4,64,128]{2,1,0:T(8,128)(2,1)S(1)}, u32[]{:S(2)}, u32[]{:S(2)}) collective-permute-start(bf16[4,64,128]{2,1,0:T(8,128)(2,1)S(1)} %slice.158), channel_id=1, source_target_pairs={{0,16},{4,20},{8,24},{12,28},{16,0},{20,4},{24,8},{28,12},{1,17},{... | collective-permute-start | bytes 196616 | tf_op jit(solution)/shard_map/ppermute | solution.py:19
  (1 other events, 0.9 us)
